TPU v7x, 128 devices: a whole 4x4x4 slice. The times are simulated.
128 devices in a mesh: layer: 32 (over x_hi, y, z), cuts: 4 (over x_lo, core).
Axes of the slice: x: 4 (x_hi: 2, x_lo: 2; x = x_hi * 2 + x_lo), y: 4, z: 4, core: 2. Of those that a mesh axis runs over, the one named last changes fastest.
Arguments:
- resid: bfloat16 [512, 2, 16384], P(None, None, 'cuts'), may hold values from -6 to 6
- enc_weight: bfloat16 [2, 16384, 8192], P(None, 'cuts', 'layer'), may hold values from -0.03125 to 0.03125
- enc_bias: float32 [8192], P('layer'), may hold values from -1 to 1
- dec_weight: bfloat16 [8192, 2, 16384], P('layer', None, 'cuts'), may hold values from -0.09375 to 0.09375
- dec_bias: float32 [2, 16384], P(None, 'cuts'), may hold values from -1 to 1
Outputs:
- enc_grad: bfloat16 [2, 16384, 8192], P(None, 'cuts', 'layer')
- dec_grad: bfloat16 [8192, 2, 16384], P('layer', None, 'cuts')
All inputs are finite; a program needn't handle non-finite values.
Results may differ from a plain program's by a relative error of at most 0.012.
Values may be sent and summed in bfloat16 or wider, within the bound.
A program may use at most 128 MiB of HBM per device.

v0:
```python
import math
import jax
import jax.numpy as jnp
from jax import lax
from jax.sharding import PartitionSpec as P


def copy_for_each(x, axis):
    copies = jnp.broadcast_to(x, (lax.axis_size(axis), *x.shape))
    return lax.all_to_all(copies, axis, split_axis=0, concat_axis=0, tiled=True)


def taken_together(x, axis):
    everything = copy_for_each(x, axis)
    return jnp.sum(everything, axis=0)


def filled_up(lines, size):
    spare = -len(lines) % size
    return jnp.pad(lines, [(0, spare)] + [(0, 0)] * (lines.ndim - 1))


def sum_by_parts(x, axis):
    lines = x.reshape(-1, *x.shape[1:][-1:])
    padded = filled_up(lines, lax.axis_size(axis))
    own = lax.psum_scatter(padded, axis, scatter_dimension=0, tiled=True)
    whole = lax.all_gather(own, axis, axis=0, tiled=True)
    return whole[: len(lines)].reshape(x.shape)


def per_device(resid, enc_weight, enc_bias, dec_weight, dec_bias):
    rows = resid.shape[0]
    local = resid.reshape(rows, -1)
    width = local.shape[1]
    encoder = enc_weight.reshape(width, -1)
    feats = encoder.shape[1]
    decoder = dec_weight.reshape(feats, width)
    offset = dec_bias.reshape(-1)
    scale = 1.0 / math.sqrt(rows)
    groups = lax.axis_size("layer")
    partial_sum = jnp.dot(local, encoder, preferred_element_type=jnp.float32)
    z_local = taken_together(partial_sum, "cuts") + enc_bias[None, :]
    act = jnp.maximum(z_local, 0.0).astype(jnp.bfloat16)
    share = rows // groups
    block = act
    recon = lax.psum_scatter(
        jnp.dot(block, decoder, preferred_element_type=jnp.float32),
        "layer",
        scatter_dimension=0,
        tiled=True,
    )
    mine = lax.axis_index("layer") * share
    own_rows = lax.dynamic_slice_in_dim(local, mine, share, 0)
    err = (recon + offset[None, :] - own_rows.astype(jnp.float32)).astype(jnp.bfloat16)
    piece = lax.all_gather(err, "layer", axis=0, tiled=True)
    block = act
    grad = lax.dot_general(
        block, piece, (((0,), (0,)), ((), ())), preferred_element_type=jnp.float32
    )
    values = lax.dot_general(
        piece, decoder, (((1,), (1,)), ((), ())), preferred_element_type=jnp.float32
    )
    dact = values
    grad, dact = (grad, dact)
    dec_grad = (grad * scale).astype(jnp.bfloat16)
    back = sum_by_parts(dact, "cuts")
    masked = jnp.where(z_local > 0, back * scale, 0.0).astype(jnp.bfloat16)
    enc_full = lax.dot_general(
        local, masked, (((0,), (0,)), ((), ())), preferred_element_type=jnp.float32
    )
    enc_grad = enc_full.astype(jnp.bfloat16).reshape(enc_weight.shape)
    return (enc_grad, dec_grad.reshape(dec_weight.shape))


def solution(mesh):
    placed = (
        P(None, None, "cuts"),
        P(None, "cuts", "layer"),
        P("layer"),
        P("layer", None, "cuts"),
        P(None, "cuts"),
    )
    return jax.shard_map(
        per_device,
        mesh=mesh,
        in_specs=placed,
        out_specs=(P(None, "cuts", "layer"), P("layer", None, "cuts")),
        check_vma=False,
    )
```

profile of v0, /device:TPU:1, one launch (start us, length us, event | category | flops | bytes accessed | tf_op | source)
XLA Modules:
  0.0 445.2 jit_solution(11260148202417527209)
XLA Ops:
  7.2 9.3 %fusion.4 = f32[512,256]{1,0:T(8,128)S(1)} fusion(bf16[2,4096,256]{2,1,0:T(8,128)(2,1)} %param.6, bf16[512,2,4096]{2,1,0:T(2,128)(2,1)} %param.5), kind=kOutput, calls=%fused_computation.6 | convolution fusion | flops 2147483648 | bytes 13107200 | tf_op jit(solution)/shard_map/dot_general | solution.py:41
  16.5 0.0 copy-start
  16.5 1.5 broadcast_in_dim.6
  18.0 5.0 %all-to-all-start = ((f32[4,512,256]{2,1,0:T(8,128)}), f32[4,512,256]{2,1,0:T(8,128)S(1)}, u32[]{:S(2)}, u32[]{:S(2)}) async-start(f32[4,512,256]{2,1,0:T(8,128)} %broadcast_in_dim.6), calls=%async_computation | async-start | bytes 4194304 | tf_op jit(solution)/shard_map/all_to_all | solution.py:10
  22.9 0.0 reduce-scatter.3.cloned.1.call-start
  22.9 8.7 %copy.12 = bf16[32,8,2,4096]{3,1,2,0:T(8,128)(2,1)} copy(bf16[32,8,2,4096]{3,2,1,0:T(2,128)(2,1)} %bitcast.22) | data formatting | bytes 8388608
  31.6 16.0 %all-to-all-done = f32[4,512,256]{2,1,0:T(8,128)S(1)} async-done(((f32[4,512,256]{2,1,0:T(8,128)}), f32[4,512,256]{2,1,0:T(8,128)S(1)}, u32[]{:S(2)}, u32[]{:S(2)}) %all-to-all-start) | async-done | bytes 2097184 | tf_op jit(solution)/shard_map/all_to_all | solution.py:10
  47.6 0.2 reduce_sum.9
  47.8 0.0 copy-done
  47.8 10.3 %fusion.10 = f32[512,8192]{1,0:T(8,128)} fusion(bf16[256,8192]{1,0:T(8,128)(2,1)} %bitcast.19, f32[512,256]{1,0:T(8,128)S(1)} %reduce_sum.9, f32[256]{0:T(256)S(1)} %copy-done), kind=kOutput, calls=%fused_computation.13 | convolution fusion | flops 2147876864 | bytes 21496832 | tf_op jit(solution)/shard_map/dot_general | solution.py:47
  58.1 0.0 reduce-scatter.3.cloned.1.call-update
  58.1 0.3 all-gather.2.cloned.1.call-start
  58.4 0.0 copy-start.1
  58.4 16.2 %copy.14 = bf16[64,8,2,4096]{3,1,2,0:T(8,128)(2,1)} copy(bf16[64,8,2,4096]{3,2,1,0:T(2,128)(2,1)} %bitcast.21) | data formatting | bytes 16777216
  74.6 0.0 copy-done.1
  74.6 194.2 %reduce-scatter.3.cloned.1.call-done = f32[16,8192]{1,0:T(8,128)} async-done(((f32[512,8192]{1,0:T(8,128)}), f32[16,8192]{1,0:T(8,128)}) %reduce-scatter.3.cloned.1.call-update) | async-done | bytes 524304 | tf_op jit(solution)/shard_map/reduce_scatter | solution.py:46
  268.8 1.9 subtract_convert_fusion
  270.7 0.0 all-gather.2.cloned.1.call-update
  270.7 0.3 reduce-scatter.5.cloned.1.call-start
  271.0 120.5 %all-gather.2.cloned.1.call-done = bf16[512,8192]{1,0:T(8,128)(2,1)} async-done(((bf16[16,8192]{1,0:T(8,128)(2,1)}), bf16[512,8192]{1,0:T(8,128)(2,1)}) %all-gather.2.cloned.1.call-update) | async-done | bytes 8388624 | tf_op jit(solution)/shard_map/all_gather | solution.py:55
  391.6 7.8 %fusion.15 = f32[512,256]{1,0:T(8,128)} fusion(bf16[512,8192]{1,0:T(8,128)(2,1)} %all-gather.2.cloned.1.call-done, bf16[256,8192]{1,0:T(8,128)(2,1)} %bitcast.20), kind=kOutput, calls=%fused_computation.18 | convolution fusion | flops 2147483648 | bytes 13107200 | tf_op jit(solution)/shard_map/dot_general | solution.py:60
  399.3 0.0 reduce-scatter.5.cloned.1.call-update
  399.4 7.8 %fusion = bf16[256,8192]{1,0:T(8,128)(2,1)} fusion(bf16[512,8192]{1,0:T(8,128)(2,1)} %all-gather.2.cloned.1.call-done, f32[512,256]{1,0:T(8,128)S(1)} %reduce_sum.9, f32[256]{0:T(256)S(1)} %copy-done), kind=kOutput, calls=%fused_computation.1 | convolution fusion | flops 2152071168 | bytes 13108224 | tf_op jit(solution)/shard_map/dot_general | solution.py:57
  407.2 7.8 %reshape.22 = bf16[256,2,4096]{2,1,0:T(2,128)(2,1)} reshape(bf16[256,8192]{1,0:T(8,128)(2,1)} %fusion) | data formatting | bytes 8388608 | tf_op jit(solution)/shard_map/reshape | solution.py:72
  415.0 2.1 reduce-scatter.5.cloned.1.call-done
  417.1 7.5 %all_gather.7 = f32[512,256]{1,0:T(8,128)S(1)} all-gather(f32[128,256]{1,0:T(8,128)} %reduce-scatter.5.cloned.1.call-done), channel_id=1, replica_groups=mesh['layer'=32,'cuts'=4] {'cuts'}, dimensions={0}, use_global_device_ids=true | all-gather | bytes 655360 | tf_op jit(solution)/shard_map/all_gather | solution.py:27
  424.5 7.8 %fusion.1 = bf16[8192,256]{0,1:T(8,128)(2,1)} fusion(bf16[512,8192]{1,0:T(8,128)(2,1)} %bitcast.18, f32[512,256]{1,0:T(8,128)S(1)} %all_gather.7, f32[512,256]{1,0:T(8,128)S(1)} %reduce_sum.9, f32[256]{0:T(256)S(1)} %copy-done), kind=kOutput, calls=%fused_computation.3 | convolution fusion | flops 2150236160 | bytes 13632512 | tf_op jit(solution)/shard_map/dot_general | solution.py:68
  432.3 6.4 %copy.11 = bf16[8192,256]{1,0:T(8,128)(2,1)} copy(bf16[8192,256]{0,1:T(8,128)(2,1)} %fusion.1) | data formatting | bytes 8388608
  (1 shorter events, 0.0 us)
Async XLA Ops:
  16.5 31.3 %copy-start = (f32[256]{0:T(256)S(1)}, f32[256]{0:T(256)}, u32[]{:S(2)}) copy-start(f32[256]{0:T(256)} %param.7) | copy-start | bytes 3076
  18.0 29.7 %all-to-all-start = ((f32[4,512,256]{2,1,0:T(8,128)}), f32[4,512,256]{2,1,0:T(8,128)S(1)}, u32[]{:S(2)}, u32[]{:S(2)}) async-start(f32[4,512,256]{2,1,0:T(8,128)} %broadcast_in_dim.6), calls=%async_computation | async-start | bytes 4194304 | tf_op jit(solution)/shard_map/all_to_all | solution.py:10
  22.9 245.9 %reduce-scatter.3.cloned.1.call-start = ((), (), s32[]{:S(2)}) async-start(), calls=%async_computation.3 | async-start | bytes 17301504 | tf_op jit(solution)/shard_map/reduce_scatter | solution.py:46
  58.1 333.4 %all-gather.2.cloned.1.call-start = ((), (), s32[]{:S(2)}) async-start(), calls=%async_computation.4 | async-start | bytes 8650752 | tf_op jit(solution)/shard_map/all_gather | solution.py:55
  58.4 16.2 %copy-start.1 = (f32[2,4096]{1,0:T(2,128)S(1)}, f32[2,4096]{1,0:T(2,128)}, u32[]{:S(2)}) copy-start(f32[2,4096]{1,0:T(2,128)} %param.9) | copy-start | bytes 98308
  270.7 146.3 %reduce-scatter.5.cloned.1.call-start = ((), (), s32[]{:S(2)}) async-start(), calls=%async_computation.5 | async-start | bytes 655360 | tf_op jit(solution)/shard_map/reduce_scatter | solution.py:26
Sparse Core Ops, SparseCore 0:
  58.2 210.5 reduce-scatter.2
  272.6 118.9 all-gather.1
  399.5 17.5 reduce-scatter.4
where the time goes:
time: 446 us; the launch traced here: 445 us
  waiting for transfers between devices  333 us (75%)
  matrix products  42.9 us (10%)
  local copies, waits for them, and re-layouts  40.6 us (9%)
  between operations  13.8 us (3%)
  blocking collectives  7.48 us (2%)
  starting transfers between devices  5.52 us (1%)
    reduce_scatter x1, waiting for transfers between devices, per_device(): lax.psum_scatter(jnp.dot(block, decoder, preferred_element_type=jnp.float...  194 us
    all_gather x1, waiting for transfers between devices, per_device(): piece = lax.all_gather(err, 'layer', axis=0, tiled=True)  121 us
    unnamed x8, local copies, waits for them, and re-layouts  31.3 us
    all_to_all x1, waiting for transfers between devices, copy_for_each(): return lax.all_to_all(copies, axis, split_axis=0, concat_axis=0, tiled=True)  16 us
    dot_general x1, matrix products, per_device(): jnp.dot(block, decoder, preferred_element_type=jnp.float32)  10.3 us
    dot_general x1, matrix products, per_device(): partial_sum = jnp.dot(local, encoder, preferred_element_type=jnp.float32)  9.32 us
  transfers between devices with their start and end apart: 4, of which 4 were waited for; matrix products, arithmetic and copies ran while one was open for 9% of the time, Pallas kernels for 0%

commit v1 on v0

--- a/solution.py
+++ b/solution.py
@@ -52,7 +52,9 @@
     mine = lax.axis_index("layer") * share
     own_rows = lax.dynamic_slice_in_dim(local, mine, share, 0)
     err = (recon + offset[None, :] - own_rows.astype(jnp.float32)).astype(jnp.bfloat16)
-    piece = lax.all_gather(err, "layer", axis=0, tiled=True)
+    piece = jnp.concatenate(
+        lax.all_to_all(jnp.stack([err] * lax.axis_size("layer")), "layer", 0, 0), axis=0
+    )
     block = act
     grad = lax.dot_general(
         block, piece, (((0,), (0,)), ((), ())), preferred_element_type=jnp.float32

time: 446 us -> 426 us (0.955)
  waiting for transfers between devices: 333 us -> 243 us
  blocking collectives: 7.48 us -> 78.6 us
  matrix products: 42.9 us -> 38.3 us
    all_gather x1 -> x0, waiting for transfers between devices: 121 us -> none  [per_device(): piece = lax.all_gather(err, 'layer', axis=0, tiled=True)]
    all_to_all x0 -> x1, blocking collectives: none -> 71.1 us  [per_device(): lax.all_to_all(jnp.stack([err] * lax.axis_size('layer')), 'layer', 0, 0)]
    reduce_scatter x1, waiting for transfers between devices: 2.08 us -> 32.7 us  [sum_by_parts(): own = lax.psum_scatter(padded, axis, scatter_dimension=0, tiled=True)]
    dot_general x1, matrix products: 7.78 us -> 3.19 us  [per_device(): lax.dot_general(piece, decoder, (((1,), (1,)), ((), ())), preferred_eleme...]
    unnamed x8 -> x12, local copies, waits for them, and re-layouts: 31.3 us -> 34.5 us
  transfers between devices with their start and end apart: 4 -> 3, of which waited for: 4 -> 3; matrix products, arithmetic and copies ran while one was open for 9% -> 10% of each run, Pallas kernels for 0% -> 0%
where the time goes in v1:
time: 426 us; the launch traced here: 425 us
  waiting for transfers between devices  243 us (57%)
  blocking collectives  78.6 us (18%)
  local copies, waits for them, and re-layouts  44.8 us (11%)
  matrix products  38.3 us (9%)
  between operations  14.1 us (3%)
  starting transfers between devices  5.22 us (1%)
    reduce_scatter x1, waiting for transfers between devices, per_device(): lax.psum_scatter(jnp.dot(block, decoder, preferred_element_type=jnp.float...  194 us
    all_to_all x1, blocking collectives, per_device(): lax.all_to_all(jnp.stack([err] * lax.axis_size('layer')), 'layer', 0, 0)  71.1 us
    unnamed x12, local copies, waits for them, and re-layouts  34.5 us
    reduce_scatter x1, waiting for transfers between devices, sum_by_parts(): own = lax.psum_scatter(padded, axis, scatter_dimension=0, tiled=True)  32.7 us
    all_to_all x1, waiting for transfers between devices, copy_for_each(): return lax.all_to_all(copies, axis, split_axis=0, concat_axis=0, tiled=True)  16 us
    dot_general x1, matrix products, per_device(): jnp.dot(block, decoder, preferred_element_type=jnp.float32)  10.3 us
    dot_general x1, matrix products, per_device(): partial_sum = jnp.dot(local, encoder, preferred_element_type=jnp.float32)  9.32 us
  transfers between devices with their start and end apart: 3, of which 3 were waited for; matrix products, arithmetic and copies ran while one was open for 10% of the time, Pallas kernels for 0%

profile of v1, /device:TPU:1, one launch (start us, length us, event | category | flops | bytes accessed | tf_op | source)
XLA Modules:
  0.0 425.3 jit_solution(1135299239164200467)
XLA Ops:
  7.2 9.3 %fusion.4 = f32[512,256]{1,0:T(8,128)S(1)} fusion(bf16[2,4096,256]{2,1,0:T(8,128)(2,1)} %param.6, bf16[512,2,4096]{2,1,0:T(2,128)(2,1)} %param.5), kind=kOutput, calls=%fused_computation.6 | convolution fusion | flops 2147483648 | bytes 13107200 | tf_op jit(solution)/shard_map/dot_general | solution.py:41
  16.5 0.0 copy-start.2
  16.5 1.5 broadcast_in_dim.6
  18.0 5.0 %all-to-all-start = ((f32[4,512,256]{2,1,0:T(8,128)}), f32[4,512,256]{2,1,0:T(8,128)S(1)}, u32[]{:S(2)}, u32[]{:S(2)}) async-start(f32[4,512,256]{2,1,0:T(8,128)} %broadcast_in_dim.6), calls=%async_computation | async-start | bytes 4194304 | tf_op jit(solution)/shard_map/all_to_all | solution.py:10
  22.9 0.0 reduce-scatter.3.cloned.1.call-start
  22.9 8.7 %copy.12 = bf16[32,8,2,4096]{3,1,2,0:T(8,128)(2,1)} copy(bf16[32,8,2,4096]{3,2,1,0:T(2,128)(2,1)} %bitcast.25) | data formatting | bytes 8388608
  31.6 16.0 %all-to-all-done = f32[4,512,256]{2,1,0:T(8,128)S(1)} async-done(((f32[4,512,256]{2,1,0:T(8,128)}), f32[4,512,256]{2,1,0:T(8,128)S(1)}, u32[]{:S(2)}, u32[]{:S(2)}) %all-to-all-start) | async-done | bytes 2097184 | tf_op jit(solution)/shard_map/all_to_all | solution.py:10
  47.6 0.2 reduce_sum.9
  47.8 0.0 copy-done.2
  47.8 10.3 %fusion.10 = f32[512,8192]{1,0:T(8,128)} fusion(bf16[256,8192]{1,0:T(8,128)(2,1)} %bitcast.22, f32[512,256]{1,0:T(8,128)S(1)} %reduce_sum.9, f32[256]{0:T(256)S(1)} %copy-done.2), kind=kOutput, calls=%fused_computation.13 | convolution fusion | flops 2147876864 | bytes 21496832 | tf_op jit(solution)/shard_map/dot_general | solution.py:47
  58.1 0.0 reduce-scatter.3.cloned.1.call-update
  58.1 0.3 reduce-scatter.5.cloned.1.call-start
  58.4 0.0 copy-start.3
  58.4 16.2 %copy.14 = bf16[64,8,2,4096]{3,1,2,0:T(8,128)(2,1)} copy(bf16[64,8,2,4096]{3,2,1,0:T(2,128)(2,1)} %bitcast.24) | data formatting | bytes 16777216
  74.6 0.0 copy-done.3
  74.6 194.2 %reduce-scatter.3.cloned.1.call-done = f32[16,8192]{1,0:T(8,128)} async-done(((f32[512,8192]{1,0:T(8,128)}), f32[16,8192]{1,0:T(8,128)}) %reduce-scatter.3.cloned.1.call-update) | async-done | bytes 524304 | tf_op jit(solution)/shard_map/reduce_scatter | solution.py:46
  268.8 1.2 subtract_convert_fusion
  270.0 1.0 stack.2
  271.0 0.0 copy-start.1
  271.0 71.1 %all_to_all.10 = bf16[32,16,8192]{2,1,0:T(8,128)(2,1)S(1)} all-to-all(bf16[32,16,8192]{2,1,0:T(8,128)(2,1)S(1)} %stack.2), channel_id=1, replica_groups=mesh['layer'=32,'cuts'=4] {'layer'}, dimensions={0} | all-to-all | bytes 16777216 | tf_op jit(solution)/shard_map/all_to_all | solution.py:56
  342.2 0.0 copy-start
  342.2 3.2 copy-done
  345.4 0.0 copy-done.1
  345.4 3.2 fusion.15
  348.6 0.0 reduce-scatter.5.cloned.1.call-update
  348.6 7.8 %fusion = bf16[256,8192]{1,0:T(8,128)(2,1)} fusion(bf16[512,8192]{1,0:T(8,128)(2,1)} %bitcast.21, f32[512,256]{1,0:T(8,128)S(1)} %reduce_sum.9, f32[256]{0:T(256)S(1)} %copy-done.2), kind=kOutput, calls=%fused_computation.1 | convolution fusion | flops 2152071168 | bytes 13108224 | tf_op jit(solution)/shard_map/dot_general | solution.py:59
  356.4 7.8 %reshape.28 = bf16[256,2,4096]{2,1,0:T(2,128)(2,1)} reshape(bf16[256,8192]{1,0:T(8,128)(2,1)} %fusion) | data formatting | bytes 8388608 | tf_op jit(solution)/shard_map/reshape | solution.py:74
  364.2 32.7 %reduce-scatter.5.cloned.1.call-done = f32[128,256]{1,0:T(8,128)} async-done(((f32[512,256]{1,0:T(8,128)}), f32[128,256]{1,0:T(8,128)}) %reduce-scatter.5.cloned.1.call-update) | async-done | bytes 131088 | tf_op jit(solution)/shard_map/reduce_scatter | solution.py:26
  396.9 7.5 %all_gather.3 = f32[512,256]{1,0:T(8,128)S(1)} all-gather(f32[128,256]{1,0:T(8,128)} %reduce-scatter.5.cloned.1.call-done), channel_id=1, replica_groups=mesh['layer'=32,'cuts'=4] {'cuts'}, dimensions={0}, use_global_device_ids=true | all-gather | bytes 655360 | tf_op jit(solution)/shard_map/all_gather | solution.py:27
  404.4 7.8 %fusion.1 = bf16[8192,256]{0,1:T(8,128)(2,1)} fusion(bf16[512,8192]{1,0:T(8,128)(2,1)} %bitcast.19, f32[512,256]{1,0:T(8,128)S(1)} %all_gather.3, f32[512,256]{1,0:T(8,128)S(1)} %reduce_sum.9, f32[256]{0:T(256)S(1)} %copy-done.2), kind=kOutput, calls=%fused_computation.3 | convolution fusion | flops 2150236160 | bytes 13632512 | tf_op jit(solution)/shard_map/dot_general | solution.py:70
  412.1 6.4 %copy.11 = bf16[8192,256]{1,0:T(8,128)(2,1)} copy(bf16[8192,256]{0,1:T(8,128)(2,1)} %fusion.1) | data formatting | bytes 8388608
  (1 shorter events, 0.0 us)
Async XLA Ops:
  16.5 31.3 %copy-start.2 = (f32[256]{0:T(256)S(1)}, f32[256]{0:T(256)}, u32[]{:S(2)}) copy-start(f32[256]{0:T(256)} %param.7) | copy-start | bytes 3076
  18.0 29.7 %all-to-all-start = ((f32[4,512,256]{2,1,0:T(8,128)}), f32[4,512,256]{2,1,0:T(8,128)S(1)}, u32[]{:S(2)}, u32[]{:S(2)}) async-start(f32[4,512,256]{2,1,0:T(8,128)} %broadcast_in_dim.6), calls=%async_computation | async-start | bytes 4194304 | tf_op jit(solution)/shard_map/all_to_all | solution.py:10
  22.9 245.9 %reduce-scatter.3.cloned.1.call-start = ((), (), s32[]{:S(2)}) async-start(), calls=%async_computation.4 | async-start | bytes 17301504 | tf_op jit(solution)/shard_map/reduce_scatter | solution.py:46
  58.1 338.8 %reduce-scatter.5.cloned.1.call-start = ((), (), s32[]{:S(2)}) async-start(), calls=%async_computation.5 | async-start | bytes 655360 | tf_op jit(solution)/shard_map/reduce_scatter | solution.py:26
  58.4 16.2 %copy-start.3 = (f32[2,4096]{1,0:T(2,128)S(1)}, f32[2,4096]{1,0:T(2,128)}, u32[]{:S(2)}) copy-start(f32[2,4096]{1,0:T(2,128)} %param.9) | copy-start | bytes 98308
  271.0 74.4 %copy-start.1 = (bf16[32,8,2,4096]{3,1,2,0:T(8,128)(2,1)S(1)}, bf16[32,8,2,4096]{3,1,2,0:T(8,128)(2,1)}, u32[]{:S(2)}) copy-start(bf16[32,8,2,4096]{3,1,2,0:T(8,128)(2,1)} %copy.12) | copy-start | bytes 12582916
  342.2 3.2 copy-start
Sparse Core Ops, SparseCore 0:
  58.2 210.5 reduce-scatter.2
  348.7 48.1 reduce-scatter.4
